TPU v7x, 32 devices: a whole 2x2x4 slice. The times are simulated.
32 devices in a mesh: date: 4 (over y, x), pix: 8 (over z, core).
Axes of the slice: x: 2, y: 2, z: 4, core: 2. Of those that a mesh axis runs over, the one named last changes fastest.
Arguments:
- stack: bfloat16 [64, 7, 64, 1024], P('date', None, None, 'pix'), may hold values from -8 to 8
- quality: int32 [64, 64, 1024], P('date', None, 'pix'), may hold values from 0 to 1073741823
- days: int32 [64], P('date'), may hold values from 8 to 1536, as said below
Outputs:
- coef: float32 [7, 8, 64, 1024], P(None, None, 'pix', 'date')
- score: float32 [7, 64, 1024], P(None, 'pix', 'date')
Inputs may be any that keep to these rules, and one draw needn't show every extreme that they name: `days`: strictly increasing.
All inputs are finite; a program needn't handle non-finite values.
Results may differ from a plain program's by a relative error of at most 0.0003.
Values may be sent and summed in bfloat16 or wider, within the bound.
A program may use at most 256 MiB of HBM per device.

v0:
```python
import jax
import jax.numpy as jnp
from jax import lax
from jax.sharding import PartitionSpec as P

RIDGE_TERM = 1.0
PAIR_LIST = [(first, second) for first in range(8) for second in range(first, 8)]


def pair_number(first, second):
    return PAIR_LIST.index((min(first, second), max(first, second)))


def design_matrix(days):
    moment_t = days.astype(jnp.float32)
    columns = [jnp.ones_like(moment_t), (moment_t - 512.0) / 512.0]
    for order in range(1, 4):
        phase = 2.0 * jnp.pi * order * moment_t / 365.25
        columns.append(jnp.cos(phase))
        columns.append(jnp.sin(phase))
    return jnp.stack(columns, 1)


def weights(quality):
    cloud = jnp.bitwise_and(jnp.right_shift(quality, 3), 1)
    level = jnp.bitwise_and(jnp.right_shift(quality, 8), 3)
    return (1 - cloud).astype(jnp.float32) / (1.0 + level.astype(jnp.float32))


def pair_products(design):
    return jnp.stack([design[:, first] * design[:, second] for first, second in PAIR_LIST], 1)


def chol_solve(gram, moment):
    lower = {}
    for first in range(8):
        for second in range(first + 1):
            total = gram[pair_number(first, second)]
            if first == second:
                total = total + RIDGE_TERM
            for inner in range(second):
                total = total - lower[first, inner] * lower[second, inner]
            if first == second:
                lower[first, first] = jnp.sqrt(total)
            else:
                lower[first, second] = total / lower[second, second]
    forward = []
    for first in range(8):
        total = moment[first]
        for inner in range(first):
            total = total - lower[first, inner][None, :] * forward[inner]
        forward.append(total / lower[first, first][None, :])
    backward = [None] * 8
    for first in range(7, -1, -1):
        total = forward[first]
        for inner in range(first + 1, 8):
            total = total - lower[inner, first][None, :] * backward[inner]
        backward[first] = total / lower[first, first][None, :]
    return jnp.stack(backward, 0)


def local(stack, quality, days):
    high = lax.Precision.HIGHEST
    bands = stack.shape[1]
    local_dates, all_rows, arrive_cols = (stack.shape[0], stack.shape[2], stack.shape[3])
    arrive_pixels = all_rows * arrive_cols
    design = design_matrix(days)
    weight = weights(quality).reshape(local_dates, arrive_pixels)
    samples = stack.reshape(local_dates, bands, arrive_pixels).astype(jnp.float32)
    gram_part = jnp.dot(pair_products(design).T, weight, precision=high)
    weighted = weight[:, None, :] * samples
    moment_part = jnp.dot(
        design.T, weighted.reshape(local_dates, bands * arrive_pixels), precision=high
    )
    square_part = jnp.sum(weighted * samples, 0)
    weight_part = jnp.sum(weight, 0)[None, :]
    stacked = jnp.concatenate(
        [gram_part, moment_part.reshape(8 * bands, arrive_pixels), square_part, weight_part], 0
    )
    stacked = stacked.reshape(stacked.shape[0], all_rows, arrive_cols)
    spread = lax.all_to_all(stacked, "pix", split_axis=1, concat_axis=2, tiled=True)
    summed = lax.psum_scatter(spread, "date", scatter_dimension=2, tiled=True)
    row_count, col_count = (summed.shape[1], summed.shape[2])
    pixels = row_count * col_count
    summed = summed.reshape(summed.shape[0], pixels)
    gram = summed[:36]
    moment = summed[36 : 36 + 8 * bands].reshape(8, bands, pixels)
    squares = summed[36 + 8 * bands : 36 + 9 * bands]
    wsum = summed[36 + 9 * bands]
    coef_flat = chol_solve(gram, moment)
    ssr = squares - 2.0 * jnp.sum(coef_flat * moment, 0)
    for first in range(8):
        for second in range(8):
            ssr = (
                ssr
                + gram[pair_number(first, second)][None, :] * coef_flat[first] * coef_flat[second]
            )
    total_ssr, total_weight = lax.psum((jnp.sum(ssr, 1), jnp.sum(wsum)), ("date", "pix"))
    sigma2 = total_ssr / total_weight
    score = jnp.sqrt(ssr / (wsum[None, :] + 1.0)) / jnp.sqrt(sigma2)[:, None]
    coef = jnp.transpose(coef_flat.reshape(8, bands, row_count, col_count), (1, 0, 2, 3))
    return (coef, score.reshape(bands, row_count, col_count))


def solution(mesh):
    return jax.shard_map(
        local,
        mesh=mesh,
        in_specs=(P("date", None, None, "pix"), P("date", None, "pix"), P("date")),
        out_specs=(P(None, None, "pix", "date"), P(None, "pix", "date")),
        check_vma=False,
    )
```

profile of v0, /device:TPU:0, one launch (start us, length us, event | category | flops | bytes accessed | tf_op | source)
XLA Modules:
  0.0 227.7 jit_solution(3004523274341131072)
XLA Ops:
  7.2 1.2 fusion.103
  8.5 2.0 fusion
  11.3 0.3 copy.246
  11.6 0.4 mul.6375
  12.0 3.9 %copy.189 = f32[2,8,7,8192]{3,1,2,0:T(8,128)} copy(f32[2,8,7,8192]{3,2,1,0:T(8,128)S(1)} %bitcast.504) | data formatting | bytes 7340032
  15.9 2.2 convert.1
  18.2 8.7 %fusion.1 = f32[8,57344]{1,0:T(8,128)} fusion(f32[16,8]{1,0:T(8,128)S(1)} %stack.167, f32[16,57344]{1,0:T(8,128)} %bitcast.505, f32[2,8,448,128]{3,2,1,0:T(8,128)} %convert.1), kind=kOutput, calls=%fused_computation.3 | convolution fusion | flops 88997888 | bytes 9175552 | tf_op jit(solution)/shard_map/dot_general | solution.py:72
  26.9 1.8 concatenate.9
  28.7 2.3 %copy.183 = f32[56,64,128]{2,0,1:T(8,128)} copy(f32[56,64,128]{2,1,0:T(8,128)S(1)} %concatenate.9) | data formatting | bytes 3670016 | tf_op jit(solution)/shard_map/concatenate | solution.py:77
  33.5 1.2 fusion.3
  34.8 0.3 pad_maximum_fusion
  35.1 83.3 %all_to_all.18 = f32[100,64,128]{2,0,1:T(8,128)S(1)} all-to-all(f32[100,64,128]{2,0,1:T(8,128)S(1)} %pad_maximum_fusion), channel_id=1, replica_groups=mesh['date'=4,'pix'=8] {'pix'}, dimensions={1} | all-to-all | bytes 6553600 | tf_op jit(solution)/shard_map/all_to_all | solution.py:81
  118.4 2.3 copy.245
  120.7 44.1 %reduce-scatter.2.cloned.1.call-done = f32[100,8,256]{2,1,0:T(8,128)} async-done(((f32[100,8,1024]{2,1,0:T(8,128)}), f32[100,8,256]{2,1,0:T(8,128)}) %reduce-scatter.2.cloned.1.call-update) | async-done | bytes 819216 | tf_op jit(solution)/shard_map/reduce_scatter | solution.py:82
  164.8 0.9 add_bitcast_fusion
  165.7 1.5 slice_reduce_fusion
  167.6 0.9 fusion.104
  168.6 0.8 rsqrt_multiply_fusion.39
  169.4 0.9 rsqrt_multiply_fusion.28
  170.3 0.9 rsqrt_multiply_fusion.26
  171.1 0.9 rsqrt_multiply_fusion.27
  172.0 0.7 rsqrt_multiply_fusion.40
  172.7 0.8 rsqrt_multiply_fusion.18
  173.5 0.8 subtract_sqrt_fusion.7
  174.3 0.8 rsqrt_multiply_fusion.10
  175.1 0.8 subtract_sqrt_fusion.6
  176.7 0.4 divide_dynamic-update-slice_fusion
  178.0 0.9 fusion.93
  179.2 0.8 copy.186
  180.0 39.5 %all-reduce = (f32[7]{0:T(128)S(1)}, f32[]{:T(128)}) all-reduce(f32[7]{0:T(128)S(1)} %get-tuple-element.12, f32[]{:T(128)} %get-tuple-element.192), channel_id=1, replica_groups=mesh['date'=4,'pix'=8] {'date','pix'}, use_global_device_ids=true, to_apply=%region_5.0 | all-reduce | flops 8 | bytes 64 | tf_op jit(solution)/shard_map/psum | solution.py:98
  219.5 0.7 divide_sqrt_fusion
  220.2 0.7 sqrt_divide_fusion
  (130 shorter events, 5.3 us)
Async XLA Ops:
  7.2 3.5 %copy-start.3 = (s32[16]{0:T(128)S(1)}, s32[16]{0:T(128)}, u32[]{:S(2)}) copy-start(s32[16]{0:T(128)} %param.5) | copy-start | bytes 196
  7.2 157.6 %reduce-scatter.2.cloned.1.call-start = ((), (), s32[]{:S(2)}) async-start(), calls=%async_computation.2 | async-start | bytes 4096000 | tf_op jit(solution)/shard_map/reduce_scatter | solution.py:82
  12.0 3.9 %copy-start.1 = (bf16[16,7,64,128]{3,2,1,0:T(8,128)(2,1)S(1)}, bf16[16,7,64,128]{3,2,1,0:T(8,128)(2,1)}, u32[]{:S(2)}) copy-start(bf16[16,7,64,128]{3,2,1,0:T(8,128)(2,1)} %param.3) | copy-start | bytes 5505028
  31.0 3.7 %copy-start.2 = (f32[56,64,128]{2,0,1:T(8,128)S(1)}, f32[56,64,128]{2,0,1:T(8,128)}, u32[]{:S(2)}) copy-start(f32[56,64,128]{2,0,1:T(8,128)} %copy.183) | copy-start | bytes 5505028
  164.8 11.1 %copy-start = (f32[100,8,256]{2,1,0:T(8,128)S(1)}, f32[100,8,256]{2,1,0:T(8,128)}, u32[]{:S(2)}) copy-start(f32[100,8,256]{2,1,0:T(8,128)} %reduce-scatter.2.cloned.1.call-done) | copy-start | bytes 2457604
  176.3 1.4 slice-start
Sparse Core Ops, SparseCore 0:
  120.8 43.9 reduce-scatter.1
where the time goes:
time: 229 us; the launch traced here: 228 us
  blocking collectives  123 us (54%)
  waiting for transfers between devices  44.1 us (19%)
  other arithmetic  19.6 us (9%)
  local copies, waits for them, and re-layouts  16.5 us (7%)
  between operations  14.7 us (6%)
  matrix products  9.93 us (4%)
    all_to_all x1, blocking collectives, local(): lax.all_to_all(stacked, 'pix', split_axis=1, concat_axis=2, tiled=True)  83.3 us
    reduce_scatter x1, waiting for transfers between devices, local(): summed = lax.psum_scatter(spread, 'date', scatter_dimension=2, tiled=True)  44.1 us
    psum x1, blocking collectives, local(): lax.psum((jnp.sum(ssr, 1), jnp.sum(wsum)), ('date', 'pix'))  39.5 us
    dot_general x1, matrix products, local(): jnp.dot(design.T, weighted.reshape(local_dates, bands * arrive_pixels), p...  8.69 us
    div x14, other arithmetic, chol_solve(): lower[first, second] = total / lower[second, second]  5.87 us
    unnamed x54, local copies, waits for them, and re-layouts  5.3 us
  transfers between devices with their start and end apart: 1, of which 1 were waited for; matrix products, arithmetic and copies ran while one was open for 0% of the time, Pallas kernels for 0%

commit v1 on v0

v1 whole, which is shorter than its diff:
```python
import functools

import jax
import jax.numpy as jnp
from jax import lax
from jax.experimental import pallas as pl
from jax.experimental.pallas import tpu as pltpu
from jax.sharding import PartitionSpec as P

RIDGE_TERM = 1.0
HARM = 8
LAG = 2
MESH = pl.DeviceIdType.MESH
PAIR_LIST = [(first, second) for first in range(HARM) for second in range(first + 1)]
PAIR_AT = {pair: number for number, pair in enumerate(PAIR_LIST)}


def design_matrix(days):
    moment_t = days.astype(jnp.float32)
    columns = [jnp.ones_like(moment_t), (moment_t - 512.0) / 512.0]
    for order in range(1, 4):
        phase = 2.0 * jnp.pi * order * moment_t / 365.25
        columns.append(jnp.cos(phase))
        columns.append(jnp.sin(phase))
    return jnp.stack(columns, 1)


def kernel(dims, stack, quality, des_in, coef, score,
           qbuf, code, raw, dall, bdes, wbuf, lbuf, wsum_ref, res, rel, fin,
           ssum, part, part_date, part_mid, part_pix,
           q_sem, des_send, des_recv, raw_send, raw_recv,
           hop_send, rel_recv, fin_send, fin_recv,
           pd_send, pd_recv, pp_send, pp_recv):
    dates, pixes, times, bands, block = dims
    per = pixes // dates
    s = lax.axis_index("date")
    q = lax.axis_index("pix")
    total = dates * times
    home = q // per

    def target(sd, j):
        return per * lax.rem(sd + per * lax.rem(q, 2) + j, dates) + j

    def owner(qq, p):
        shift = per * lax.rem(qq, 2) + lax.rem(p, per)
        return lax.rem(p // per + 64 * dates - shift, dates)

    barrier = pltpu.get_barrier_semaphore()
    for k in range(1, dates):
        pl.semaphore_signal(barrier, inc=1, device_id=(lax.rem(s + k, dates), q),
                            device_id_type=MESH)
    for k in range(1, pixes):
        pl.semaphore_signal(barrier, inc=1, device_id=(s, lax.rem(q + k, pixes)),
                            device_id_type=MESH)

    q_copy = pltpu.make_async_copy(quality, qbuf, q_sem)
    q_copy.start()

    def own_copy(j, b):
        rows = pl.ds(pl.multiple_of(target(s, j) * block, block), block)
        return pltpu.make_async_copy(
            stack.at[:, b, rows, :], raw.at[j, b, pl.ds(s * times, times)],
            raw_recv.at[j, b, s])

    def own_code(j):
        return pltpu.make_async_copy(
            code.at[target(s, j)], raw.at[j, bands, pl.ds(s * times, times)],
            raw_recv.at[j, bands, s])

    for j in range(per):
        for b in range(bands):
            own_copy(j, b).start()

    q_copy.wait()
    for p in range(pixes):
        bits = qbuf[:, p * block:(p + 1) * block, :]
        cloud = jnp.bitwise_and(jnp.right_shift(bits, 3), 1)
        level = jnp.bitwise_and(jnp.right_shift(bits, 8), 3)
        code[p] = ((1 - cloud) * (1 + level)).astype(jnp.float32).astype(jnp.bfloat16)

    pl.semaphore_wait(barrier, dates - 1 + pixes - 1)

    def des_copy(k):
        return pltpu.make_async_remote_copy(
            des_in, dall.at[s], des_send.at[k], des_recv.at[s],
            device_id=(lax.rem(s + k, dates), q), device_id_type=MESH)

    def raw_copy(j, b, k):
        peer = lax.rem(s + k, dates)
        rows = pl.ds(pl.multiple_of(target(peer, j) * block, block), block)
        return pltpu.make_async_remote_copy(
            stack.at[:, b, rows, :], raw.at[j, b, pl.ds(s * times, times)],
            raw_send.at[j, b, k], raw_recv.at[j, b, s],
            device_id=(peer, q), device_id_type=MESH)

    def code_copy(j, k):
        peer = lax.rem(s + k, dates)
        return pltpu.make_async_remote_copy(
            code.at[target(peer, j)], raw.at[j, bands, pl.ds(s * times, times)],
            raw_send.at[j, bands, k], raw_recv.at[j, bands, s],
            device_id=(peer, q), device_id_type=MESH)

    for k in range(1, dates):
        des_copy(k).start()
    for j in range(per):
        own_code(j).start()
        for k in range(1, dates):
            code_copy(j, k).start()
    for j in range(per):
        for b in range(bands):
            for k in range(1, dates):
                raw_copy(j, b, k).start()

    def raw_wait(j, b, sd):
        pltpu.make_async_copy(
            raw.at[j, b, pl.ds(sd * times, times)],
            raw.at[j, b, pl.ds(sd * times, times)],
            raw_recv.at[j, b, sd]).wait()

    dall[s] = des_in[...]
    for k in range(1, dates):
        sd = lax.rem(s + k, dates)
        pltpu.make_async_copy(dall.at[sd], dall.at[sd], des_recv.at[sd]).wait()

    @pl.loop(0, total)
    def _(t):
        row = dall[t // times, pl.ds(lax.rem(t, times), 1), :]
        for i in range(HARM):
            bdes[t, i] = jnp.broadcast_to(row[:, i:i + 1], (block, 128))

    zero = jnp.zeros((block, 128), jnp.float32)
    for b in range(bands + 1):
        ssum[b] = zero

    def gram_step(j):
        for sd in range(dates):
            raw_wait(j, bands, sd)

        def body(t, carry):
            value = raw[j, bands, t].astype(jnp.float32)
            w = jnp.where(value == 0.0, 0.0, 1.0 / jnp.maximum(value, 1.0))
            wbuf[t] = w
            d = [bdes[t, i] for i in range(HARM)]
            wd = [w] + [w * d[i] for i in range(1, HARM)]
            return tuple(
                carry[n] + (wd[first] if second == 0 else wd[first] * d[second])
                for n, (first, second) in enumerate(PAIR_LIST))

        gram = lax.fori_loop(0, total, body, (zero,) * len(PAIR_LIST), unroll=2)
        wsum_ref[...] = gram[0]
        ssum[bands] = ssum[bands] + gram[0]
        lower = {}
        for first in range(HARM):
            for second in range(first + 1):
                value = gram[PAIR_AT[first, second]]
                if first == second:
                    value = value + RIDGE_TERM
                for inner in range(second):
                    value = value - lower[first, inner] * lower[second, inner]
                if first == second:
                    lower[first, first] = 1.0 / jnp.sqrt(value)
                else:
                    lower[first, second] = value * lower[second, second]
                lbuf[PAIR_AT[first, second]] = lower[first, second]

    def hop(j, b, start):
        p = target(s, j)

        def act(dst, sem):
            @pl.when(p != q)
            def _():
                c = pltpu.make_async_remote_copy(
                    res.at[j, b], dst, hop_send.at[j, b], sem,
                    device_id=(s, p), device_id_type=MESH)
                c.start() if start else c.wait_send()

            if start:
                @pl.when(p == q)
                def _():
                    pltpu.make_async_copy(res.at[j, b], dst, sem).start()

        @pl.when(home == s)
        def _():
            act(fin.at[lax.rem(q, per), b], fin_recv.at[lax.rem(q, per), b])

        @pl.when(home != s)
        def _():
            act(rel.at[q, b], rel_recv.at[q, b])

    def band_step(j, b):
        for sd in range(dates):
            raw_wait(j, b, sd)

        def body(t, carry):
            wy = wbuf[t] * raw[j, b, t].astype(jnp.float32)
            return tuple(
                carry[i] + (wy if i == 0 else bdes[t, i] * wy) for i in range(HARM))

        moment = lax.fori_loop(0, total, body, (zero,) * HARM, unroll=8)
        low = lambda first, second: lbuf[PAIR_AT[first, second]]
        forward = []
        for first in range(HARM):
            value = moment[first]
            for inner in range(first):
                value = value - low(first, inner) * forward[inner]
            forward.append(value * low(first, first))
        back = [None] * HARM
        for first in range(HARM - 1, -1, -1):
            value = forward[first]
            for inner in range(HARM - 1, first, -1):
                value = value - low(inner, first) * back[inner]
            back[first] = value * low(first, first)
        for i in range(HARM):
            res[j, b, i] = back[i]

        def residual(t, ssr):
            terms = [back[0]] + [bdes[t, i] * back[i] for i in range(1, HARM)]
            while len(terms) > 1:
                terms = [terms[i] + terms[i + 1] for i in range(0, len(terms), 2)]
            diff = raw[j, b, t].astype(jnp.float32) - terms[0]
            return ssr + wbuf[t] * diff * diff

        ssr = lax.fori_loop(0, total, residual, zero, unroll=8)
        res[j, b, HARM] = jnp.sqrt(ssr / (wsum_ref[...] + 1.0))
        ssum[b] = ssum[b] + ssr
        hop(j, b, True)

    def pass_on(qq, b, start):
        far = qq // per

        @pl.when(jnp.logical_and(owner(qq, q) == s, far != s))
        def _():
            c = pltpu.make_async_remote_copy(
                rel.at[qq, b], fin.at[lax.rem(qq, per), b], fin_send.at[qq, b],
                fin_recv.at[lax.rem(qq, per), b],
                device_id=(far, q), device_id_type=MESH)
            if start:
                pltpu.make_async_copy(rel.at[qq, b], rel.at[qq, b], rel_recv.at[qq, b]).wait()
                c.start()
            else:
                c.wait_send()

    def relay(n):
        b = lax.rem(n, bands)

        @pl.when(n // bands == lax.rem(q, per))
        def _():
            @pl.loop(0, pixes)
            def _(qq):
                pass_on(qq, b, True)

    @pl.loop(0, per * bands)
    def _(n):
        j = n // bands
        b = lax.rem(n, bands)

        @pl.when(b == 0)
        def _():
            gram_step(j)

        band_step(j, b)

        @pl.when(n >= LAG)
        def _():
            relay(n - LAG)

    part[...] = jnp.concatenate(
        [jnp.sum(ssum[b], 0, keepdims=True) for b in range(bands + 1)], 0)

    def date_part(k):
        return pltpu.make_async_remote_copy(
            part, part_date.at[s], pd_send.at[k], pd_recv.at[s],
            device_id=(lax.rem(s + k, dates), q), device_id_type=MESH)

    def pix_part(k):
        return pltpu.make_async_remote_copy(
            part_mid, part_pix.at[q], pp_send.at[k], pp_recv.at[q],
            device_id=(s, lax.rem(q + k, pixes)), device_id_type=MESH)

    for k in range(1, dates):
        date_part(k).start()
    part_date[s] = part[...]
    for n in range(LAG):
        relay(per * bands - LAG + n)
    for k in range(1, dates):
        sd = lax.rem(s + k, dates)
        pltpu.make_async_copy(part_date.at[sd], part_date.at[sd], pd_recv.at[sd]).wait()
    mid = part_date[0]
    for sd in range(1, dates):
        mid = mid + part_date[sd]
    part_mid[...] = mid
    for k in range(1, pixes):
        pix_part(k).start()
    part_pix[q] = mid

    @pl.loop(0, bands)
    def _(b):
        for c in range(per):
            pltpu.make_async_copy(fin.at[c, b], fin.at[c, b], fin_recv.at[c, b]).wait()
            for i in range(HARM):
                coef[b, i, :, c * 128:(c + 1) * 128] = fin[c, b, i]

    for k in range(1, pixes):
        qq = lax.rem(q + k, pixes)
        pltpu.make_async_copy(part_pix.at[qq], part_pix.at[qq], pp_recv.at[qq]).wait()
    tot = part_pix[0]
    for qq in range(1, pixes):
        tot = tot + part_pix[qq]
    tot = jnp.sum(tot, 1, keepdims=True)
    for b in range(bands):
        sigma = jnp.sqrt(tot[b:b + 1] / tot[bands:bands + 1])
        sigma = jnp.broadcast_to(sigma, (block, 128))
        for c in range(per):
            score[b, :, c * 128:(c + 1) * 128] = fin[c, b, HARM] / sigma

    for k in range(1, dates):
        des_copy(k).wait_send()
        date_part(k).wait_send()
    for k in range(1, pixes):
        pix_part(k).wait_send()

    @pl.loop(0, per)
    def _(j):
        for k in range(1, dates):
            code_copy(j, k).wait_send()

        @pl.loop(0, bands)
        def _(b):
            for k in range(1, dates):
                raw_copy(j, b, k).wait_send()
            hop(j, b, False)

    @pl.loop(0, pixes)
    def _(qq):
        @pl.loop(0, bands)
        def _(b):
            pass_on(qq, b, False)


def local(mesh, stack, quality, days):
    dates, pixes = mesh.shape["date"], mesh.shape["pix"]
    times, bands, rows, width = stack.shape
    block = rows // pixes
    per = pixes // dates
    total = dates * times
    des = jnp.pad(design_matrix(days), ((0, 0), (0, 128 - HARM)))
    dims = (dates, pixes, times, bands, block)
    tile = (block, width)
    vmem, dma = pltpu.VMEM, pltpu.SemaphoreType.DMA
    f32, bf16 = jnp.float32, jnp.bfloat16
    return pl.pallas_call(
        functools.partial(kernel, dims),
        out_shape=(
            jax.ShapeDtypeStruct((bands, HARM, block, width * per), f32),
            jax.ShapeDtypeStruct((bands, block, width * per), f32),
        ),
        in_specs=[
            pl.BlockSpec(memory_space=pl.ANY),
            pl.BlockSpec(memory_space=pl.ANY),
            pl.BlockSpec(memory_space=pltpu.VMEM),
        ],
        out_specs=(
            pl.BlockSpec(memory_space=pltpu.VMEM),
            pl.BlockSpec(memory_space=pltpu.VMEM),
        ),
        scratch_shapes=[
            vmem((times, rows, width), jnp.int32),
            vmem((pixes, times) + tile, bf16),
            vmem((per, bands + 1, total) + tile, bf16),
            vmem((dates, times, 128), f32),
            vmem((total, HARM) + tile, f32),
            vmem((total,) + tile, f32),
            vmem((len(PAIR_LIST),) + tile, f32),
            vmem(tile, f32),
            vmem((per, bands, HARM + 1) + tile, f32),
            vmem((pixes, bands, HARM + 1) + tile, f32),
            vmem((per, bands, HARM + 1) + tile, f32),
            vmem((bands + 1,) + tile, f32),
            vmem((bands + 1, width), f32),
            vmem((dates, bands + 1, width), f32),
            vmem((bands + 1, width), f32),
            vmem((pixes, bands + 1, width), f32),
            dma,
            dma((dates,)),
            dma((dates,)),
            dma((per, bands + 1, dates)),
            dma((per, bands + 1, dates)),
            dma((per, bands)),
            dma((pixes, bands)),
            dma((pixes, bands)),
            dma((per, bands)),
            dma((dates,)),
            dma((dates,)),
            dma((pixes,)),
            dma((pixes,)),
        ],
        compiler_params=pltpu.CompilerParams(
            collective_id=0, has_side_effects=True, vmem_limit_bytes=60000000
        ),
    )(stack, quality, des)


def solution(mesh):
    return jax.shard_map(
        functools.partial(local, mesh),
        mesh=mesh,
        in_specs=(P("date", None, None, "pix"), P("date", None, "pix"), P("date")),
        out_specs=(P(None, None, "pix", "date"), P(None, "pix", "date")),
        check_vma=False,
    )
```

time: 229 us -> 53 us (0.23)
  blocking collectives: 123 us -> 0 us
  Pallas kernels: 0 us -> 46.8 us
  waiting for transfers between devices: 44.1 us -> 0 us
  other arithmetic: 19.6 us -> 0.71 us
  between operations: 14.7 us -> 0.65 us
  local copies, waits for them, and re-layouts: 16.5 us -> 4.54 us
  matrix products: 9.93 us -> 0 us
    all_to_all x1 -> x0, blocking collectives: 83.3 us -> none  [local(): lax.all_to_all(stacked, 'pix', split_axis=1, concat_axis=2, tiled=True)]
    pallas_call x0 -> x1, Pallas kernels: none -> 46.8 us  [local(): pl.pallas_call(functools.partial(kernel, dims), out_shape=(jax.ShapeDtype...]
    reduce_scatter x1 -> x0, waiting for transfers between devices: 44.1 us -> none  [local(): summed = lax.psum_scatter(spread, 'date', scatter_dimension=2, tiled=True)]
    psum x1 -> x0, blocking collectives: 39.5 us -> none  [local(): lax.psum((jnp.sum(ssr, 1), jnp.sum(wsum)), ('date', 'pix'))]
    dot_general x2 -> x0, matrix products: 9.93 us -> none  [the longest x1 8.69 us: local(): jnp.dot(design.T, weighted.reshape(local_dates, bands * arrive_pixels), p...]
    div x16 -> x0, other arithmetic: 6.64 us -> none  [the longest x14 5.87 us: chol_solve(): lower[first, second] = total / lower[second, second]]
    reduce_sum x5 -> x0, other arithmetic: 5.69 us -> none  [the longest x1 2.01 us: local(): square_part = jnp.sum(weighted * samples, 0)]
    concatenate x2 -> x0, local copies, waits for them, and re-layouts: 4.09 us -> none  [local(): jnp.concatenate([gram_part, moment_part.reshape(8 * bands, arrive_pixels)...]
  transfers between devices with their start and end apart: 1 -> 0, of which waited for: 1 -> 0; matrix products, arithmetic and copies ran while one was open for 0% -> 0% of each run, Pallas kernels for 0% -> 0%
where the time goes in v1:
time: 53 us; the launch traced here: 52.7 us
  Pallas kernels  46.8 us (88%)
  local copies, waits for them, and re-layouts  4.54 us (9%)
  other arithmetic  0.71 us (1%)
  between operations  0.65 us (1%)
    pallas_call x1, Pallas kernels, local(): pl.pallas_call(functools.partial(kernel, dims), out_shape=(jax.ShapeDtype...  46.8 us
    unnamed x2, local copies, waits for them, and re-layouts  3.27 us

profile of v1, /device:TPU:0, one launch (start us, length us, event | category | flops | bytes accessed | tf_op | source)
XLA Modules:
  0.0 52.7 jit_solution(11167647683733396907)
XLA Ops:
  0.6 0.7 %sine_bitcast_fusion = (f32[16,1]{0,1:T(1,128)S(1)}, f32[16,1]{0,1:T(1,128)S(1)}, f32[16,1]{0,1:T(1,128)S(1)}, f32[16,1]{0,1:T(1,128)S(1)}, f32[16,1]{0,1:T(1,12...) fusion(s32[16]{0:T(128)} %param.5), kind=kLoop, calls=%fused_computation | loop fusion | flops 96 | bytes 512 | tf_op jit(solution)/shard_map/stack | solution.py:25
  1.3 0.1 copy.11
  1.4 0.1 copy.9
  1.5 0.1 copy.7
  1.6 0.1 copy.6
  1.7 0.1 copy.8
  1.8 0.1 copy.10
  1.8 0.1 copy.5
  1.9 0.1 stack.32
  2.0 0.6 %pad.4.des_in = f32[16,128]{1,0:T(8,128)} pad(f32[16,8]{1,0:T(8,128)S(1)} %stack.32, f32[]{:T(128)} %constant.22.clone.1), padding=0_0x0_120 | pad | bytes 8708 | tf_op jit(solution)/shard_map/jit(_pad)/pad | solution.py:346
  2.6 46.8 %shard_map.50 = (f32[7,8,8,256]{3,2,1,0:T(8,128)}, f32[7,8,256]{2,1,0:T(8,128)}) custom-call(bf16[16,7,64,128]{3,2,1,0:T(8,128)(2,1)} %stack.33, s32[16,64,128]{2,1,0:T(8,128)} %quality.1, f32[16,128]{1,0:T(8,128)} %pad.4.des_in), custom_call_target="tpu_custom_call" | custom-call | tf_op jit(solution)/shard_map/pallas_call | solution.py:351
  49.5 1.8 %copy.14 = f32[7,8,8,256]{3,2,1,0:T(8,128)} copy(f32[7,8,8,256]{3,2,1,0:T(8,128)} %get-tuple-element.11) | data formatting | bytes 917504
  51.3 1.4 %copy.15 = f32[7,8,256]{2,1,0:T(8,128)} copy(f32[7,8,256]{2,1,0:T(8,128)} %get-tuple-element.12) | data formatting | bytes 114688
  (1 shorter events, 0.0 us)

commit v2 on v1

--- a/solution.py
+++ b/solution.py
@@ -15,18 +15,20 @@
 PAIR_AT = {pair: number for number, pair in enumerate(PAIR_LIST)}
 
 
-def design_matrix(days):
-    moment_t = days.astype(jnp.float32)
-    columns = [jnp.ones_like(moment_t), (moment_t - 512.0) / 512.0]
-    for order in range(1, 4):
-        phase = 2.0 * jnp.pi * order * moment_t / 365.25
-        columns.append(jnp.cos(phase))
-        columns.append(jnp.sin(phase))
-    return jnp.stack(columns, 1)
-
-
-def kernel(dims, stack, quality, des_in, coef, score,
-           qbuf, code, raw, dall, bdes, wbuf, lbuf, wsum_ref, res, rel, fin,
+def design_lanes(days):
+    rows = [jnp.full((1, 128), day, jnp.int32) for day in days]
+    moment_t = jnp.concatenate(rows, 0).astype(jnp.float32)
+    lane = lax.broadcasted_iota(jnp.int32, moment_t.shape, 1)
+    rate = jnp.where(
+        lane < 4, 2.0 * jnp.pi, jnp.where(lane < 6, 4.0 * jnp.pi, 6.0 * jnp.pi))
+    phase = rate * moment_t / 365.25
+    wave = jnp.where(jnp.bitwise_and(lane, 1) == 0, jnp.cos(phase), jnp.sin(phase))
+    linear = (moment_t - 512.0) / 512.0
+    return jnp.where(lane == 0, 1.0, jnp.where(lane == 1, linear, wave))
+
+
+def kernel(dims, stack, quality, days, fin, tot_ref,
+           des_in, qbuf, code, raw, dall, bdes, wbuf, lbuf, wsum_ref, res, rel,
            ssum, part, part_date, part_mid, part_pix,
            q_sem, des_send, des_recv, raw_send, raw_recv,
            hop_send, rel_recv, fin_send, fin_recv,
@@ -36,6 +38,12 @@
     s = lax.axis_index("date")
     q = lax.axis_index("pix")
     total = dates * times
+
+    def peer_of(k):
+        if dates & (dates - 1):
+            return lax.rem(s + k, dates)
+        return jnp.bitwise_xor(s, k)
+
     home = q // per
 
     def target(sd, j):
@@ -47,7 +55,7 @@
 
     barrier = pltpu.get_barrier_semaphore()
     for k in range(1, dates):
-        pl.semaphore_signal(barrier, inc=1, device_id=(lax.rem(s + k, dates), q),
+        pl.semaphore_signal(barrier, inc=1, device_id=(peer_of(k), q),
                             device_id_type=MESH)
     for k in range(1, pixes):
         pl.semaphore_signal(barrier, inc=1, device_id=(s, lax.rem(q + k, pixes)),
@@ -71,6 +79,7 @@
         for b in range(bands):
             own_copy(j, b).start()
 
+    des_in[...] = design_lanes([days[r] for r in range(times)])
     q_copy.wait()
     for p in range(pixes):
         bits = qbuf[:, p * block:(p + 1) * block, :]
@@ -83,10 +92,10 @@
     def des_copy(k):
         return pltpu.make_async_remote_copy(
             des_in, dall.at[s], des_send.at[k], des_recv.at[s],
-            device_id=(lax.rem(s + k, dates), q), device_id_type=MESH)
+            device_id=(peer_of(k), q), device_id_type=MESH)
 
     def raw_copy(j, b, k):
-        peer = lax.rem(s + k, dates)
+        peer = peer_of(k)
         rows = pl.ds(pl.multiple_of(target(peer, j) * block, block), block)
         return pltpu.make_async_remote_copy(
             stack.at[:, b, rows, :], raw.at[j, b, pl.ds(s * times, times)],
@@ -94,7 +103,7 @@
             device_id=(peer, q), device_id_type=MESH)
 
     def code_copy(j, k):
-        peer = lax.rem(s + k, dates)
+        peer = peer_of(k)
         return pltpu.make_async_remote_copy(
             code.at[target(peer, j)], raw.at[j, bands, pl.ds(s * times, times)],
             raw_send.at[j, bands, k], raw_recv.at[j, bands, s],
@@ -119,10 +128,10 @@
 
     dall[s] = des_in[...]
     for k in range(1, dates):
-        sd = lax.rem(s + k, dates)
+        sd = peer_of(k)
         pltpu.make_async_copy(dall.at[sd], dall.at[sd], des_recv.at[sd]).wait()
 
-    @pl.loop(0, total)
+    @pl.loop(0, total, unroll=4)
     def _(t):
         row = dall[t // times, pl.ds(lax.rem(t, times), 1), :]
         for i in range(HARM):
@@ -270,7 +279,7 @@
     def date_part(k):
         return pltpu.make_async_remote_copy(
             part, part_date.at[s], pd_send.at[k], pd_recv.at[s],
-            device_id=(lax.rem(s + k, dates), q), device_id_type=MESH)
+            device_id=(peer_of(k), q), device_id_type=MESH)
 
     def pix_part(k):
         return pltpu.make_async_remote_copy(
@@ -283,7 +292,7 @@
     for n in range(LAG):
         relay(per * bands - LAG + n)
     for k in range(1, dates):
-        sd = lax.rem(s + k, dates)
+        sd = peer_of(k)
         pltpu.make_async_copy(part_date.at[sd], part_date.at[sd], pd_recv.at[sd]).wait()
     mid = part_date[0]
     for sd in range(1, dates):
@@ -297,8 +306,6 @@
     def _(b):
         for c in range(per):
             pltpu.make_async_copy(fin.at[c, b], fin.at[c, b], fin_recv.at[c, b]).wait()
-            for i in range(HARM):
-                coef[b, i, :, c * 128:(c + 1) * 128] = fin[c, b, i]
 
     for k in range(1, pixes):
         qq = lax.rem(q + k, pixes)
@@ -306,12 +313,7 @@
     tot = part_pix[0]
     for qq in range(1, pixes):
         tot = tot + part_pix[qq]
-    tot = jnp.sum(tot, 1, keepdims=True)
-    for b in range(bands):
-        sigma = jnp.sqrt(tot[b:b + 1] / tot[bands:bands + 1])
-        sigma = jnp.broadcast_to(sigma, (block, 128))
-        for c in range(per):
-            score[b, :, c * 128:(c + 1) * 128] = fin[c, b, HARM] / sigma
+    tot_ref[...] = tot
 
     for k in range(1, dates):
         des_copy(k).wait_send()
@@ -335,6 +337,19 @@
         @pl.loop(0, bands)
         def _(b):
             pass_on(qq, b, False)
+
+
+def finish(fin, tot_ref, coef, score):
+    per, bands = fin.shape[:2]
+    tot = jnp.sum(tot_ref[...], 1, keepdims=True)
+    for b in range(bands):
+        sigma = jnp.sqrt(tot[b:b + 1] / tot[bands:bands + 1])
+        scale = jnp.broadcast_to(1.0 / sigma, fin.shape[3:])
+        for c in range(per):
+            cols = slice(c * 128, (c + 1) * 128)
+            for i in range(HARM):
+                coef[b, i, :, cols] = fin[c, b, i]
+            score[b, :, cols] = fin[c, b, HARM] * scale
 
 
 def local(mesh, stack, quality, days):
@@ -343,27 +358,27 @@
     block = rows // pixes
     per = pixes // dates
     total = dates * times
-    des = jnp.pad(design_matrix(days), ((0, 0), (0, 128 - HARM)))
     dims = (dates, pixes, times, bands, block)
     tile = (block, width)
     vmem, dma = pltpu.VMEM, pltpu.SemaphoreType.DMA
     f32, bf16 = jnp.float32, jnp.bfloat16
-    return pl.pallas_call(
+    fin, tot = pl.pallas_call(
         functools.partial(kernel, dims),
         out_shape=(
-            jax.ShapeDtypeStruct((bands, HARM, block, width * per), f32),
-            jax.ShapeDtypeStruct((bands, block, width * per), f32),
+            jax.ShapeDtypeStruct((per, bands, HARM + 1) + tile, f32),
+            jax.ShapeDtypeStruct((bands + 1, width), f32),
         ),
         in_specs=[
             pl.BlockSpec(memory_space=pl.ANY),
             pl.BlockSpec(memory_space=pl.ANY),
-            pl.BlockSpec(memory_space=pltpu.VMEM),
+            pl.BlockSpec(memory_space=pltpu.SMEM),
         ],
         out_specs=(
-            pl.BlockSpec(memory_space=pltpu.VMEM),
+            pl.BlockSpec(memory_space=pl.ANY),
             pl.BlockSpec(memory_space=pltpu.VMEM),
         ),
         scratch_shapes=[
+            vmem((times, 128), f32),
             vmem((times, rows, width), jnp.int32),
             vmem((pixes, times) + tile, bf16),
             vmem((per, bands + 1, total) + tile, bf16),
@@ -374,7 +389,6 @@
             vmem(tile, f32),
             vmem((per, bands, HARM + 1) + tile, f32),
             vmem((pixes, bands, HARM + 1) + tile, f32),
-            vmem((per, bands, HARM + 1) + tile, f32),
             vmem((bands + 1,) + tile, f32),
             vmem((bands + 1, width), f32),
             vmem((dates, bands + 1, width), f32),
@@ -397,7 +411,17 @@
         compiler_params=pltpu.CompilerParams(
             collective_id=0, has_side_effects=True, vmem_limit_bytes=60000000
         ),
-    )(stack, quality, des)
+    )(stack, quality, days)
+    whole = pl.BlockSpec(memory_space=pltpu.VMEM)
+    return pl.pallas_call(
+        finish,
+        out_shape=(
+            jax.ShapeDtypeStruct((bands, HARM, block, width * per), f32),
+            jax.ShapeDtypeStruct((bands, block, width * per), f32),
+        ),
+        in_specs=[whole, whole],
+        out_specs=(whole, whole),
+    )(fin, tot)
 
 
 def solution(mesh):

time: 53 us -> 47.7 us (0.900)
  local copies, waits for them, and re-layouts: 4.54 us -> 0 us
  other arithmetic: 0.71 us -> 0 us
    unnamed x2 -> x0, local copies, waits for them, and re-layouts: 3.27 us -> none
    pallas_call x0 -> x1, Pallas kernels: none -> 1.85 us  [local(): pl.pallas_call(finish, out_shape=(jax.ShapeDtypeStruct((bands, HARM, bloc...]
    pallas_call x1, Pallas kernels: 46.8 us -> 45.1 us  [local(): pl.pallas_call(functools.partial(kernel, dims), out_shape=(jax.ShapeDtype...]
    another operation x1 -> x0, other arithmetic: 0.71 us -> none  [design_matrix(): return jnp.stack(columns, 1)]
    another operation x9 -> x0, local copies, waits for them, and re-layouts: 0.67 us -> none  [the longest x8 0.66 us: design_matrix(): return jnp.stack(columns, 1)]
    pad x1 -> x0, local copies, waits for them, and re-layouts: 0.61 us -> none  [local(): des = jnp.pad(design_matrix(days), ((0, 0), (0, 128 - HARM)))]
where the time goes in v2:
time: 47.7 us; the launch traced here: 47.6 us
  Pallas kernels  46.9 us (98%)
  between operations  0.64 us (1%)
    pallas_call x1, Pallas kernels, local(): pl.pallas_call(functools.partial(kernel, dims), out_shape=(jax.ShapeDtype...  45.1 us
    pallas_call x1, Pallas kernels, local(): pl.pallas_call(finish, out_shape=(jax.ShapeDtypeStruct((bands, HARM, bloc...  1.85 us

profile of v2, /device:TPU:0, one launch (start us, length us, event | category | flops | bytes accessed | tf_op | source)
XLA Modules:
  0.0 47.6 jit_solution(15525594726473301620)
XLA Ops:
  0.6 45.1 %shard_map.50 = (f32[2,7,9,8,128]{4,3,2,1,0:T(8,128)}, f32[8,128]{1,0:T(8,128)}) custom-call(bf16[16,7,64,128]{3,2,1,0:T(8,128)(2,1)} %stack.1, s32[16,64,128]{2,1,0:T(8,128)} %quality.1, s32[16]{0:T(128)} %days.1), custom_call_target="tpu_custom_call" | custom-call | tf_op jit(solution)/shard_map/pallas_call | solution.py:365
  45.7 1.8 %shard_map.51 = (f32[7,8,8,256]{3,2,1,0:T(8,128)}, f32[7,8,256]{2,1,0:T(8,128)}) custom-call(f32[2,7,9,8,128]{4,3,2,1,0:T(8,128)} %get-tuple-element.4.fin, f32[8,128]{1,0:T(8,128)} %get-tuple-element.5.tot_ref), custom_call_target="tpu_custom_call" | custom-call | tf_op jit(solution)/shard_map/pallas_call | solution.py:416

commit v3 on v2

--- a/solution.py
+++ b/solution.py
@@ -9,7 +9,13 @@
 
 RIDGE_TERM = 1.0
 HARM = 8
-LAG = 2
+LAG = 4
+EARLY = 1
+LIMIT = 32767.0
+
+
+def ORDER(dates):
+    return range(dates - 1, 0, -1)
 MESH = pl.DeviceIdType.MESH
 PAIR_LIST = [(first, second) for first in range(HARM) for second in range(first + 1)]
 PAIR_AT = {pair: number for number, pair in enumerate(PAIR_LIST)}
@@ -79,6 +85,32 @@
         for b in range(bands):
             own_copy(j, b).start()
 
+    pl.semaphore_wait(barrier, dates - 1 + pixes - 1)
+
+    def des_copy(k):
+        return pltpu.make_async_remote_copy(
+            des_in, dall.at[s], des_send.at[k], des_recv.at[s],
+            device_id=(peer_of(k), q), device_id_type=MESH)
+
+    def raw_copy(j, b, k):
+        peer = peer_of(k)
+        rows = pl.ds(pl.multiple_of(target(peer, j) * block, block), block)
+        return pltpu.make_async_remote_copy(
+            stack.at[:, b, rows, :], raw.at[j, b, pl.ds(s * times, times)],
+            raw_send.at[j, b, k], raw_recv.at[j, b, s],
+            device_id=(peer, q), device_id_type=MESH)
+
+    def code_copy(j, k):
+        peer = peer_of(k)
+        return pltpu.make_async_remote_copy(
+            code.at[target(peer, j)], raw.at[j, bands, pl.ds(s * times, times)],
+            raw_send.at[j, bands, k], raw_recv.at[j, bands, s],
+            device_id=(peer, q), device_id_type=MESH)
+
+    for b in range(EARLY):
+        for k in ORDER(dates):
+            raw_copy(0, b, k).start()
+
     des_in[...] = design_lanes([days[r] for r in range(times)])
     q_copy.wait()
     for p in range(pixes):
@@ -87,28 +119,6 @@
         level = jnp.bitwise_and(jnp.right_shift(bits, 8), 3)
         code[p] = ((1 - cloud) * (1 + level)).astype(jnp.float32).astype(jnp.bfloat16)
 
-    pl.semaphore_wait(barrier, dates - 1 + pixes - 1)
-
-    def des_copy(k):
-        return pltpu.make_async_remote_copy(
-            des_in, dall.at[s], des_send.at[k], des_recv.at[s],
-            device_id=(peer_of(k), q), device_id_type=MESH)
-
-    def raw_copy(j, b, k):
-        peer = peer_of(k)
-        rows = pl.ds(pl.multiple_of(target(peer, j) * block, block), block)
-        return pltpu.make_async_remote_copy(
-            stack.at[:, b, rows, :], raw.at[j, b, pl.ds(s * times, times)],
-            raw_send.at[j, b, k], raw_recv.at[j, b, s],
-            device_id=(peer, q), device_id_type=MESH)
-
-    def code_copy(j, k):
-        peer = peer_of(k)
-        return pltpu.make_async_remote_copy(
-            code.at[target(peer, j)], raw.at[j, bands, pl.ds(s * times, times)],
-            raw_send.at[j, bands, k], raw_recv.at[j, bands, s],
-            device_id=(peer, q), device_id_type=MESH)
-
     for k in range(1, dates):
         des_copy(k).start()
     for j in range(per):
@@ -116,8 +126,8 @@
         for k in range(1, dates):
             code_copy(j, k).start()
     for j in range(per):
-        for b in range(bands):
-            for k in range(1, dates):
+        for b in range(EARLY if j == 0 else 0, bands):
+            for k in ORDER(dates):
                 raw_copy(j, b, k).start()
 
     def raw_wait(j, b, sd):
@@ -219,8 +229,13 @@
             for inner in range(HARM - 1, first, -1):
                 value = value - low(inner, first) * back[inner]
             back[first] = value * low(first, first)
+        peak = jnp.abs(back[0])
+        for i in range(1, HARM):
+            peak = jnp.maximum(peak, jnp.abs(back[i]))
+        level = power(peak)
+        inverse = jnp.exp2(-level)
         for i in range(HARM):
-            res[j, b, i] = back[i]
+            res[j, b, i] = encode(back[i], inverse)
 
         def residual(t, ssr):
             terms = [back[0]] + [bdes[t, i] * back[i] for i in range(1, HARM)]
@@ -230,7 +245,12 @@
             return ssr + wbuf[t] * diff * diff
 
         ssr = lax.fori_loop(0, total, residual, zero, unroll=8)
-        res[j, b, HARM] = jnp.sqrt(ssr / (wsum_ref[...] + 1.0))
+        ratio = jnp.sqrt(ssr / (wsum_ref[...] + 1.0))
+        ratio_level = power(ratio)
+        res[j, b, HARM] = encode(ratio, jnp.exp2(-ratio_level))
+        lane = lax.broadcasted_iota(jnp.int32, ratio.shape, 1)
+        both = jnp.where(lane == 0, level, ratio_level)
+        res[j, b, HARM + 1] = both.astype(jnp.int32).astype(jnp.int16)
         ssum[b] = ssum[b] + ssr
         hop(j, b, True)
 
@@ -339,6 +359,23 @@
             pass_on(qq, b, False)
 
 
+def power(value):
+    peak = jnp.max(jnp.max(value, 0, keepdims=True), 1, keepdims=True)
+    level = jnp.ceil(jnp.log2(jnp.maximum(peak, 1e-36)) + 0.01)
+    return jnp.broadcast_to(level, value.shape)
+
+
+def encode(value, inverse):
+    root = jnp.sqrt(jnp.minimum(jnp.abs(value) * inverse, 1.0)) * LIMIT + 0.5
+    root = jnp.floor(root)
+    return jnp.where(value < 0.0, -root, root).astype(jnp.int32).astype(jnp.int16)
+
+
+def decode(value, scale):
+    root = value.astype(jnp.int32).astype(jnp.float32) * (1.0 / LIMIT)
+    return root * jnp.abs(root) * scale
+
+
 def finish(fin, tot_ref, coef, score):
     per, bands = fin.shape[:2]
     tot = jnp.sum(tot_ref[...], 1, keepdims=True)
@@ -347,9 +384,12 @@
         scale = jnp.broadcast_to(1.0 / sigma, fin.shape[3:])
         for c in range(per):
             cols = slice(c * 128, (c + 1) * 128)
+            both = fin[c, b, HARM + 1].astype(jnp.int32).astype(jnp.float32)
+            unit = jnp.broadcast_to(jnp.exp2(both[:, 0:1]), both.shape)
+            ratio_unit = jnp.broadcast_to(jnp.exp2(both[:, 1:2]), both.shape)
             for i in range(HARM):
-                coef[b, i, :, cols] = fin[c, b, i]
-            score[b, :, cols] = fin[c, b, HARM] * scale
+                coef[b, i, :, cols] = decode(fin[c, b, i], unit)
+            score[b, :, cols] = decode(fin[c, b, HARM], ratio_unit) * scale
 
 
 def local(mesh, stack, quality, days):
@@ -365,7 +405,7 @@
     fin, tot = pl.pallas_call(
         functools.partial(kernel, dims),
         out_shape=(
-            jax.ShapeDtypeStruct((per, bands, HARM + 1) + tile, f32),
+            jax.ShapeDtypeStruct((per, bands, HARM + 2) + tile, jnp.int16),
             jax.ShapeDtypeStruct((bands + 1, width), f32),
         ),
         in_specs=[
@@ -387,8 +427,8 @@
             vmem((total,) + tile, f32),
             vmem((len(PAIR_LIST),) + tile, f32),
             vmem(tile, f32),
-            vmem((per, bands, HARM + 1) + tile, f32),
-            vmem((pixes, bands, HARM + 1) + tile, f32),
+            vmem((per, bands, HARM + 2) + tile, jnp.int16),
+            vmem((pixes, bands, HARM + 2) + tile, jnp.int16),
             vmem((bands + 1,) + tile, f32),
             vmem((bands + 1, width), f32),
             vmem((dates, bands + 1, width), f32),

time: 47.7 us -> 46 us (0.964)
  Pallas kernels: 46.9 us -> 45.2 us
    pallas_call x1, Pallas kernels: 45.1 us -> 43.3 us  [local(): pl.pallas_call(functools.partial(kernel, dims), out_shape=(jax.ShapeDtype...]
where the time goes in v3:
time: 46 us; the launch traced here: 45.8 us
  Pallas kernels  45.2 us (98%)
  between operations  0.64 us (1%)
    pallas_call x1, Pallas kernels, local(): pl.pallas_call(functools.partial(kernel, dims), out_shape=(jax.ShapeDtype...  43.3 us
    pallas_call x1, Pallas kernels, local(): pl.pallas_call(finish, out_shape=(jax.ShapeDtypeStruct((bands, HARM, bloc...  1.89 us

profile of v3, /device:TPU:0, one launch (start us, length us, event | category | flops | bytes accessed | tf_op | source)
XLA Modules:
  0.0 45.8 jit_solution(16874051362779326340)
XLA Ops:
  0.6 43.3 %shard_map.50 = (s16[2,7,10,8,128]{4,3,2,1,0:T(8,128)(2,1)}, f32[8,128]{1,0:T(8,128)}) custom-call(bf16[16,7,64,128]{3,2,1,0:T(8,128)(2,1)} %stack.1, s32[16,64,128]{2,1,0:T(8,128)} %quality.1, s32[16]{0:T(128)} %days.1), custom_call_target="tpu_custom_call" | custom-call | tf_op jit(solution)/shard_map/pallas_call | solution.py:405
  43.9 1.9 %shard_map.51 = (f32[7,8,8,256]{3,2,1,0:T(8,128)}, f32[7,8,256]{2,1,0:T(8,128)}) custom-call(s16[2,7,10,8,128]{4,3,2,1,0:T(8,128)(2,1)} %get-tuple-element.4.fin, f32[8,128]{1,0:T(8,128)} %get-tuple-element.5.tot_ref), custom_call_target="tpu_custom_call" | custom-call | tf_op jit(solution)/shard_map/pallas_call | solution.py:456
